TPU v7x, 32 devices: a whole 2x2x4 slice. The times are simulated.
32 devices in a mesh: lon: 8 (over z, x), lat: 4 (over y, core).
Axes of the slice: x: 2, y: 2, z: 4, core: 2. Of those that a mesh axis runs over, the one named last changes fastest.
Arguments:
- tracers: float32 [40, 8, 32, 1024], P(None, None, 'lat', 'lon'), may hold values from -6 to 6
- kmt: int32 [32, 1024], P('lat', 'lon'), may hold values from 0 to 8
Outputs:
- updated: float32 [40, 8, 32, 1024], P(None, None, 'lat', 'lon')
Inputs may be any that keep to these rules, and one draw needn't show every extreme that they name: Level k of column (j, i) is ocean exactly when k < kmt[j, i].
All inputs are finite; a program needn't handle non-finite values.
Results may differ from a plain program's by a relative error of at most 0.00002.
Values sent between devices are 32-bit elements; how exact they have to be, the bound alone decides.
A program may use at most 64 MiB of HBM per device.

v0:
```python
import jax
import jax.numpy as jnp
from jax import lax
from jax.sharding import PartitionSpec as P

THERMAL = 0.2
HALINE = 0.8
REDI_COEF = 0.1
SKEW_COEF = 0.05
SLOPE_MAX = 0.6
SLOPE_WIDTH = 0.2


def padded(block, sides, width, periodic):
    for axis, dim in sides:
        count = lax.axis_size(axis)
        forward = [(i, i + 1) for i in range(count - 1)]
        if periodic:
            forward.append((count - 1, 0))
        backward = [(target, source) for source, target in forward]
        low = lax.ppermute(
            lax.slice_in_dim(block, block.shape[dim] - width, None, axis=dim), axis, forward
        )
        high = lax.ppermute(lax.slice_in_dim(block, 0, width, axis=dim), axis, backward)
        block = jnp.concatenate([low, block, high], axis=dim)
    return block


def from_partner(value, axis, apart):
    mask = 2**apart
    pairs = [(source, source ^ mask) for source in range(lax.axis_size(axis))]
    return lax.ppermute(value, axis, pairs)


def taper(slope):
    return slope * 0.5 * (1.0 + jnp.tanh((SLOPE_MAX - jnp.abs(slope)) / SLOPE_WIDTH))


def pad_levels(values):
    zero_layer = jnp.zeros_like(values[..., :1, :, :])
    return jnp.concatenate([zero_layer, values, zero_layer], axis=-3)


def slope_fields(density, wet_mask):
    level_mask = wet_mask[1:] * wet_mask[:-1]
    strat = (density[1:] - density[:-1]) * level_mask
    strat_pad = pad_levels(strat)
    strat_cell = 0.5 * (strat_pad[:-1] + strat_pad[1:])
    east_mask = wet_mask[:, 1:-1, :-1] * wet_mask[:, 1:-1, 1:]
    north_mask = wet_mask[:, :-1, 1:-1] * wet_mask[:, 1:, 1:-1]
    grad_east = (density[:, 1:-1, 1:] - density[:, 1:-1, :-1]) * east_mask
    strat_east = 0.5 * (strat_cell[:, 1:-1, 1:] + strat_cell[:, 1:-1, :-1])
    slope_x = taper(grad_east / jnp.maximum(strat_east, 1.0))
    grad_north = (density[:, 1:, 1:-1] - density[:, :-1, 1:-1]) * north_mask
    strat_north = 0.5 * (strat_cell[:, 1:, 1:-1] + strat_cell[:, :-1, 1:-1])
    slope_y = taper(grad_north / jnp.maximum(strat_north, 1.0))
    cell_x = 0.5 * (slope_x[..., :-1] + slope_x[..., 1:])
    cell_y = 0.5 * (slope_y[:, :-1, :] + slope_y[:, 1:, :])
    level_x = 0.5 * (cell_x[:-1] + cell_x[1:])
    level_y = 0.5 * (cell_y[:-1] + cell_y[1:])
    return (level_mask, east_mask, north_mask, slope_x, slope_y, level_x, level_y)


def tracer_step(field, fields):
    level_mask, east_mask, north_mask, slope_x, slope_y, level_x, level_y = fields
    vert_diff = (field[..., 1:, :, :] - field[..., :-1, :, :]) * level_mask
    vert_pad = pad_levels(vert_diff)
    vert_cell = 0.5 * (vert_pad[..., :-1, :, :] + vert_pad[..., 1:, :, :])
    grad_x = (field[..., 1:-1, 1:] - field[..., 1:-1, :-1]) * east_mask
    grad_y = (field[..., 1:, 1:-1] - field[..., :-1, 1:-1]) * north_mask
    flux_x = (
        -(
            REDI_COEF * grad_x
            + (REDI_COEF - SKEW_COEF)
            * slope_x
            * 0.5
            * (vert_cell[..., 1:-1, 1:] + vert_cell[..., 1:-1, :-1])
        )
        * east_mask
    )
    flux_y = (
        -(
            REDI_COEF * grad_y
            + (REDI_COEF - SKEW_COEF)
            * slope_y
            * 0.5
            * (vert_cell[..., 1:, 1:-1] + vert_cell[..., :-1, 1:-1])
        )
        * north_mask
    )
    cell_gx = 0.5 * (grad_x[..., :-1] + grad_x[..., 1:])
    cell_gy = 0.5 * (grad_y[..., :-1, :] + grad_y[..., 1:, :])
    level_gx = 0.5 * (cell_gx[..., :-1, :, :] + cell_gx[..., 1:, :, :])
    level_gy = 0.5 * (cell_gy[..., :-1, :, :] + cell_gy[..., 1:, :, :])
    flux_z = (
        -(
            (REDI_COEF + SKEW_COEF) * (level_x * level_gx + level_y * level_gy)
            + REDI_COEF * (level_x * level_x + level_y * level_y) * vert_diff[..., 1:-1, 1:-1]
        )
        * level_mask[:, 1:-1, 1:-1]
    )
    flux_pad = pad_levels(flux_z)
    tendency = -(
        flux_x[..., 1:]
        - flux_x[..., :-1]
        + (flux_y[..., 1:, :] - flux_y[..., :-1, :])
        + (flux_pad[..., 1:, :, :] - flux_pad[..., :-1, :, :])
    )
    return field[..., 1:-1, 1:-1] + tendency


def local(tracers, kmt):
    channels = tracers.shape[0]
    levels = tracers.shape[1]
    rows_here = tracers.shape[2]
    level_index = lax.broadcasted_iota(jnp.int32, (levels,) + kmt.shape, 0)
    wet_mask = (level_index < kmt[None]).astype(jnp.float32)
    stacked = jnp.concatenate([tracers, wet_mask[None]], axis=0)
    lat_index = lax.axis_index("lat")
    at_top = lat_index == lax.axis_size("lat") - 1
    lon_wide = padded(stacked, (("lon", 3),), 1, True)
    extended = padded(lon_wide, (("lat", 2),), 1, False)
    edge_row = stacked[:, :, rows_here - 1, :]
    partner = edge_row
    for bit_index in range(lax.axis_size("lon").bit_length() - 1):
        partner = from_partner(partner, "lon", bit_index)
    mirrored = partner[..., ::-1]
    north_row = jnp.where(at_top, mirrored, extended[:, :, rows_here + 1, 1:-1])
    extended = extended.at[:, :, rows_here + 1, 1:-1].set(north_row)
    density = HALINE * extended[1] - THERMAL * extended[0]
    fields = slope_fields(density, extended[channels])
    return tracer_step(extended[:channels], fields)


def solution(mesh):
    return jax.shard_map(
        local,
        mesh=mesh,
        in_specs=(P(None, None, "lat", "lon"), P("lat", "lon")),
        out_specs=P(None, None, "lat", "lon"),
        check_vma=False,
    )
```

profile of v0, /device:TPU:1, one launch (start us, length us, event | category | flops | bytes accessed | tf_op | source)
XLA Modules:
  0.0 57.9 jit_solution(1578023485517045898)
XLA Ops:
  0.0 0.0 copy-start.1
  0.0 1.6 %copy.14 = f32[40,8,8,128]{3,1,0,2:T(8,128)S(1)} copy(f32[40,8,8,128]{3,2,1,0:T(8,128)} %param.4) | data formatting | bytes 2621440 | tf_op args[0]
  1.6 0.0 copy-done.1
  1.6 2.1 %collective-permute-start.4 = (f32[41,8,128]{2,1,0:T(8,128)S(1)}, f32[41,8,128]{2,1,0:T(8,128)}, u32[]{:S(2)}, u32[]{:S(2)}) collective-permute-start(f32[41,8,128]{2,1,0:T(8,128)S(1)} %fusion.28), channel_id=1, source_target_pairs={{0,4},{4,0},{8,12},{12,8},{16,20},{20,16},{24,28},{28,24},{1,5},{5... | collective-permute-start | bytes 503816 | tf_op jit(solution)/shard_map/ppermute | solution.py:32
  3.7 1.5 %fusion.12 = (f32[41,8,8,1]{3,1,0,2:T(8,128)}, f32[41,8,8,1]{3,1,0,2:T(8,128)S(1)}) fusion(f32[1,8,8,128]{3,1,0,2:T(8,128)S(1)} %fusion.43, f32[40,8,8,128]{3,1,0,2:T(8,128)S(1)} %copy.14), kind=kLoop, calls=%fused_computation.21 | loop fusion | flops 5248 | bytes 1364480 | tf_op jit(solution)/shard_map/concatenate | solution.py:118
  5.2 1.9 %copy.15 = f32[41,8,8,1]{0,2,3,1:T(8,128)S(1)} copy(f32[41,8,8,1]{3,1,0,2:T(8,128)} %get-tuple-element.33) | data formatting | bytes 20992 | tf_op jit(solution)/shard_map/slice | solution.py:22
  7.1 0.1 collective-permute-start
  7.2 0.7 %copy.16 = f32[41,8,8,1]{0,2,3,1:T(8,128)S(1)} copy(f32[41,8,8,1]{3,1,0,2:T(8,128)S(1)} %get-tuple-element.34) | data formatting | bytes 20992 | tf_op jit(solution)/shard_map/slice | solution.py:24
  7.9 4.2 %collective-permute-start.1 = (f32[41,8,8,1]{0,2,3,1:T(8,128)S(1)}, f32[41,8,8,1]{0,2,3,1:T(8,128)S(1)}, u32[]{:S(2)}, u32[]{:S(2)}) collective-permute-start(f32[41,8,8,1]{0,2,3,1:T(8,128)S(1)} %copy.16), channel_id=1, source_target_pairs={{4,0},{8,4},{12,8},{16,12},{20,16},{24,20},{28,24},{0,28},{5,1},{9... | collective-permute-start | bytes 31496 | tf_op jit(solution)/shard_map/ppermute | solution.py:24
  12.0 0.6 %collective-permute-done = f32[41,8,8,1]{0,2,3,1:T(8,128)S(1)} collective-permute-done((f32[41,8,8,1]{0,2,3,1:T(8,128)S(1)}, f32[41,8,8,1]{0,2,3,1:T(8,128)S(1)}, u32[]{:S(2)}, u32[]{:S(2)}) %collective-permute-start) | collective-permute-done | bytes 10528 | tf_op jit(solution)/shard_map/ppermute | solution.py:21
  12.6 0.6 %copy.17 = f32[41,8,8,1]{3,1,0,2:T(8,128)S(1)} copy(f32[41,8,8,1]{0,2,3,1:T(8,128)S(1)} %collective-permute-done) | data formatting | bytes 20992 | tf_op jit(solution)/shard_map/ppermute | solution.py:21
  13.3 0.0 collective-permute-done.1
  13.3 1.7 %copy.18 = f32[41,8,8,1]{3,1,0,2:T(8,128)} copy(f32[41,8,8,1]{0,2,3,1:T(8,128)S(1)} %collective-permute-done.1) | data formatting | bytes 20992 | tf_op jit(solution)/shard_map/ppermute | solution.py:24
  15.0 2.0 %pad_maximum_fusion.4 = (f32[41,8,1,130]{3,1,0,2:T(8,128)S(1)}, f32[41,8,1,130]{3,1,0,2:T(8,128)}) fusion(f32[41,8,8,1]{3,1,0,2:T(8,128)} %copy.18, f32[41,8,8,1]{3,1,0,2:T(8,128)S(1)} %copy.17, f32[1,8,8,128]{3,1,0,2:T(8,128)S(1)} %fusion.43, f32[40,8,8,128]{3,1,0,2:T(8,128)S(1)} %copy.14), kind=kLoop, calls=%fused_computation.45 | loop fusion | flops 255840 | bytes 1705600 | tf_op jit(solution)/shard_map/slice | solution.py:22
  17.1 4.0 %collective-permute-start.3 = (f32[41,8,1,130]{3,1,0,2:T(8,128)}, f32[41,8,1,130]{3,1,0,2:T(8,128)S(1)}, u32[]{:S(2)}, u32[]{:S(2)}) collective-permute-start(f32[41,8,1,130]{3,1,0,2:T(8,128)} %get-tuple-element.30), channel_id=1, source_target_pairs={{1,0},{2,1},{3,2},{5,4},{6,5},{7,6},{9,8},{10,9},{11,10},{13,12},{... | collective-permute-start | bytes 511688 | tf_op jit(solution)/shard_map/ppermute | solution.py:24
  21.1 3.2 %collective-permute-start.2 = (f32[41,8,1,130]{3,1,0,2:T(8,128)S(1)}, f32[41,8,1,130]{3,1,0,2:T(8,128)}, u32[]{:S(2)}, u32[]{:S(2)}) collective-permute-start(f32[41,8,1,130]{3,1,0,2:T(8,128)S(1)} %get-tuple-element.29), channel_id=1, source_target_pairs={{0,1},{1,2},{2,3},{4,5},{5,6},{6,7},{8,9},{9,10},{10,11},{12,13},{... | collective-permute-start | bytes 511688 | tf_op jit(solution)/shard_map/ppermute | solution.py:21
  24.3 0.0 collective-permute-done.4
  24.3 0.1 collective-permute-start.5
  24.4 6.3 %collective-permute-done.5 = f32[41,8,128]{2,1,0:T(8,128)} collective-permute-done((f32[41,8,128]{2,1,0:T(8,128)}, f32[41,8,128]{2,1,0:T(8,128)}, u32[]{:S(2)}, u32[]{:S(2)}) %collective-permute-start.5) | collective-permute-done | bytes 167968 | tf_op jit(solution)/shard_map/ppermute | solution.py:32
  30.7 0.7 %collective-permute-start.6 = (f32[41,8,128]{2,1,0:T(8,128)}, f32[41,8,128]{2,1,0:T(8,128)S(1)}, u32[]{:S(2)}, u32[]{:S(2)}) collective-permute-start(f32[41,8,128]{2,1,0:T(8,128)} %collective-permute-done.5), channel_id=1, source_target_pairs={{0,16},{4,20},{8,24},{12,28},{16,0},{20,4},{24,8},{28,12},{1,17},{... | collective-permute-start | bytes 503816 | tf_op jit(solution)/shard_map/ppermute | solution.py:32
  31.4 0.0 collective-permute-done.3
  31.4 0.0 copy-start
  31.4 0.0 collective-permute-done.2
  31.4 0.7 %copy-done = f32[41,8,1,130]{3,1,0,2:T(8,128)} copy-done((f32[41,8,1,130]{3,1,0,2:T(8,128)}, f32[41,8,1,130]{3,1,0,2:T(8,128)S(1)}, u32[]{:S(2)}) %copy-start) | copy-done | bytes 170584
  32.1 2.5 %pad_maximum_fusion = f32[41,8,10,130]{3,1,0,2:T(8,128)S(1)} fusion(f32[41,8,1,130]{3,1,0,2:T(8,128)S(1)} %collective-permute-done.3, f32[41,8,8,1]{3,1,0,2:T(8,128)} %copy.18, f32[1,8,8,128]{3,1,0,2:T(8,128)S(1)} %fusion.43, f32[40,8,8,128]{3,1,0,2:T(8,128)S(1)} %copy.14, f32[41,8,8,1]{3,1,0,2:T(8,128)S(1)} %copy.17, f32[41,8,1,130]{3,1,0,2:T(8,128)} %collective-permute-done.2), kind=kLoop, calls=%fused_computation | loop fusion | flops 2132000 | bytes 3411200 | tf_op jit(solution)/shard_map/concatenate | solution.py:25
  34.6 0.5 copy.19
  35.1 6.5 %collective-permute-done.6 = f32[41,8,128]{2,1,0:T(8,128)S(1)} collective-permute-done((f32[41,8,128]{2,1,0:T(8,128)}, f32[41,8,128]{2,1,0:T(8,128)S(1)}, u32[]{:S(2)}, u32[]{:S(2)}) %collective-permute-start.6) | collective-permute-done | bytes 167968 | tf_op jit(solution)/shard_map/ppermute | solution.py:32
  41.6 0.8 %rev.3 = f32[41,8,128]{2,1,0:T(8,128)} reverse(f32[41,8,128]{2,1,0:T(8,128)S(1)} %collective-permute-done.6), dimensions={2} | reverse | bytes 335872 | tf_op jit(solution)/shard_map/rev | solution.py:127
  42.4 1.1 %fusion.27 = f32[41,8,1,128]{3,1,2,0:T(8,128)S(1)} fusion(f32[41,8,128]{2,1,0:T(8,128)} %rev.3, f32[41,8,1,130]{3,1,0,2:T(8,128)} %copy-done, pred[]{:T(512)S(6)} %eq.3), kind=kLoop, calls=%fused_computation.48 | loop fusion | flops 41984 | bytes 503809 | tf_op jit(solution)/shard_map/reshape.27
  43.5 6.2 %scatter.4 = f32[41,8,10,130]{3,1,2,0:T(8,128)S(1)} dynamic-update-slice(f32[41,8,10,130]{3,1,2,0:T(8,128)S(1)} %copy.19, f32[41,8,1,128]{3,1,2,0:T(8,128)S(1)} %fusion.27, s32[]{:T(128)} %constant.68.clone.1, s32[]{:T(128)} %constant.68.clone.1, s32[]{:T(128)} %constant.69.clone.1, s32[]{:T(128)} %constant.70.clone.1) | dynamic-update-slice | bytes 335876 | tf_op jit(solution)/shard_map/scatter | solution.py:129
  49.7 0.1 broadcast_multiply_fusion
  49.9 0.1 broadcast_multiply_fusion.1
  50.0 0.5 fusion
  50.5 0.1 slice.345
  50.6 0.6 %add_multiply_fusion = f32[40,8,10,130]{3,1,2,0:T(8,128)S(1)} fusion(f32[40,7,10,130]{3,1,2,0:T(8,128)S(1)} %fusion), kind=kLoop, calls=%fused_computation.3 | loop fusion | flops 832000 | bytes 3120000 | tf_op jit(solution)/shard_map/mul | solution.py:68
  51.2 0.1 fusion.41
  51.3 1.5 %fusion.4 = (f32[40,8,8,129]{3,1,2,0:T(8,128)S(1)}, f32[40,8,8,129]{3,1,2,0:T(8,128)S(1)}) fusion(f32[40,8,10,130]{3,1,2,0:T(8,128)S(1)} %add_multiply_fusion, f32[8,8,129]{2,0,1:T(8,128)S(1)} %get-tuple-element.19, f32[8,8,129]{2,0,1:T(8,128)S(1)} %get-tuple-element.21, f32[41,8,10,130]{3,1,2,0:T(8,128)S(1)} %scatter.4), kind=kLoop, calls=%fused_computation.8 | loop fusion | flops 2641920 | bytes 7991808 | tf_op jit(solution)/shard_map/mul | solution.py:72
  52.8 1.6 %fusion.9 = (f32[40,8,9,128]{3,1,2,0:T(8,128)S(1)}, f32[40,8,9,128]{3,1,2,0:T(8,128)S(1)}) fusion(f32[40,8,10,130]{3,1,2,0:T(8,128)S(1)} %add_multiply_fusion, f32[8,9,128]{2,0,1:T(8,128)S(1)} %get-tuple-element.24, f32[8,9,128]{2,0,1:T(8,128)S(1)} %get-tuple-element.26, f32[41,8,10,130]{3,1,2,0:T(8,128)S(1)} %scatter.4), kind=kLoop, calls=%fused_computation.17 | loop fusion | flops 2949120 | bytes 8921088 | tf_op jit(solution)/shard_map/mul | solution.py:82
  54.4 0.5 fusion.19
  54.9 0.7 %fusion.15 = f32[40,7,8,128]{3,1,2,0:T(8,128)S(1)} fusion(f32[40,7,10,130]{3,1,2,0:T(8,128)S(1)} %fusion, f32[40,8,8,128]{3,1,2,0:T(8,128)S(1)} %get-tuple-element.40, f32[40,8,8,128]{3,1,2,0:T(8,128)S(1)} %get-tuple-element.41, f32[7,8,128]{2,0,1:T(8,128)S(1)} %slice.345, f32[7,8,128]{2,0,1:T(8,128)S(1)} %get-tuple-element.36, ...), kind=kLoop, calls=%fused_computation.25 | loop fusion | flops 2867200 | bytes 6995968 | tf_op jit(solution)/shard_map/mul | solution.py:96
  55.6 0.9 %fusion.25 = f32[40,8,8,128]{3,1,2,0:T(8,128)S(1)} fusion(f32[40,8,9,128]{3,1,2,0:T(8,128)S(1)} %get-tuple-element.22, f32[40,8,8,129]{3,1,2,0:T(8,128)S(1)} %get-tuple-element.17, f32[41,8,10,130]{3,1,2,0:T(8,128)S(1)} %scatter.4, f32[40,7,8,128]{3,1,2,0:T(8,128)S(1)} %fusion.15), kind=kLoop, calls=%fused_computation.40 | loop fusion | flops 2293760 | bytes 9011200 | tf_op jit(solution)/shard_map/add | solution.py:109
  56.5 1.3 %copy.20 = f32[40,8,8,128]{3,2,1,0:T(8,128)} copy(f32[40,8,8,128]{3,1,2,0:T(8,128)S(1)} %fusion.25) | data formatting | bytes 2621440 | tf_op jit(solution)/shard_map/add | solution.py:109
  (6 shorter events, 0.1 us)
Async XLA Ops:
  0.0 1.6 %copy-start.1 = (s32[8,128]{1,0:T(8,128)S(1)}, s32[8,128]{1,0:T(8,128)}, u32[]{:S(2)}) copy-start(s32[8,128]{1,0:T(8,128)} %param.5) | copy-start | bytes 12292
  1.6 22.7 %collective-permute-start.4 = (f32[41,8,128]{2,1,0:T(8,128)S(1)}, f32[41,8,128]{2,1,0:T(8,128)}, u32[]{:S(2)}, u32[]{:S(2)}) collective-permute-start(f32[41,8,128]{2,1,0:T(8,128)S(1)} %fusion.28), channel_id=1, source_target_pairs={{0,4},{4,0},{8,12},{12,8},{16,20},{20,16},{24,28},{28,24},{1,5},{5... | collective-permute-start | bytes 503816 | tf_op jit(solution)/shard_map/ppermute | solution.py:32
  7.1 5.5 %collective-permute-start = (f32[41,8,8,1]{0,2,3,1:T(8,128)S(1)}, f32[41,8,8,1]{0,2,3,1:T(8,128)S(1)}, u32[]{:S(2)}, u32[]{:S(2)}) collective-permute-start(f32[41,8,8,1]{0,2,3,1:T(8,128)S(1)} %copy.15), channel_id=1, source_target_pairs={{0,4},{4,8},{8,12},{12,16},{16,20},{20,24},{24,28},{28,0},{1,5},{5... | collective-permute-start | bytes 31496 | tf_op jit(solution)/shard_map/ppermute | solution.py:21
  7.9 5.4 %collective-permute-start.1 = (f32[41,8,8,1]{0,2,3,1:T(8,128)S(1)}, f32[41,8,8,1]{0,2,3,1:T(8,128)S(1)}, u32[]{:S(2)}, u32[]{:S(2)}) collective-permute-start(f32[41,8,8,1]{0,2,3,1:T(8,128)S(1)} %copy.16), channel_id=1, source_target_pairs={{4,0},{8,4},{12,8},{16,12},{20,16},{24,20},{28,24},{0,28},{5,1},{9... | collective-permute-start | bytes 31496 | tf_op jit(solution)/shard_map/ppermute | solution.py:24
  17.1 14.3 %collective-permute-start.3 = (f32[41,8,1,130]{3,1,0,2:T(8,128)}, f32[41,8,1,130]{3,1,0,2:T(8,128)S(1)}, u32[]{:S(2)}, u32[]{:S(2)}) collective-permute-start(f32[41,8,1,130]{3,1,0,2:T(8,128)} %get-tuple-element.30), channel_id=1, source_target_pairs={{1,0},{2,1},{3,2},{5,4},{6,5},{7,6},{9,8},{10,9},{11,10},{13,12},{... | collective-permute-start | bytes 511688 | tf_op jit(solution)/shard_map/ppermute | solution.py:24
  21.1 10.3 %collective-permute-start.2 = (f32[41,8,1,130]{3,1,0,2:T(8,128)S(1)}, f32[41,8,1,130]{3,1,0,2:T(8,128)}, u32[]{:S(2)}, u32[]{:S(2)}) collective-permute-start(f32[41,8,1,130]{3,1,0,2:T(8,128)S(1)} %get-tuple-element.29), channel_id=1, source_target_pairs={{0,1},{1,2},{2,3},{4,5},{5,6},{6,7},{8,9},{9,10},{10,11},{12,13},{... | collective-permute-start | bytes 511688 | tf_op jit(solution)/shard_map/ppermute | solution.py:21
  24.3 6.4 %collective-permute-start.5 = (f32[41,8,128]{2,1,0:T(8,128)}, f32[41,8,128]{2,1,0:T(8,128)}, u32[]{:S(2)}, u32[]{:S(2)}) collective-permute-start(f32[41,8,128]{2,1,0:T(8,128)} %collective-permute-done.4), channel_id=1, source_target_pairs={{0,8},{4,12},{8,0},{12,4},{16,24},{20,28},{24,16},{28,20},{1,9},{5... | collective-permute-start | bytes 503816 | tf_op jit(solution)/shard_map/ppermute | solution.py:32
  30.7 10.9 %collective-permute-start.6 = (f32[41,8,128]{2,1,0:T(8,128)}, f32[41,8,128]{2,1,0:T(8,128)S(1)}, u32[]{:S(2)}, u32[]{:S(2)}) collective-permute-start(f32[41,8,128]{2,1,0:T(8,128)} %collective-permute-done.5), channel_id=1, source_target_pairs={{0,16},{4,20},{8,24},{12,28},{16,0},{20,4},{24,8},{28,12},{1,17},{... | collective-permute-start | bytes 503816 | tf_op jit(solution)/shard_map/ppermute | solution.py:32
  31.4 0.7 %copy-start = (f32[41,8,1,130]{3,1,0,2:T(8,128)}, f32[41,8,1,130]{3,1,0,2:T(8,128)S(1)}, u32[]{:S(2)}) copy-start(f32[41,8,1,130]{3,1,0,2:T(8,128)S(1)} %collective-permute-done.3) | copy-start | bytes 511684
where the time goes:
time: 58.6 us; the launch traced here: 57.9 us
  local copies, waits for them, and re-layouts  16 us (27%)
  starting transfers between devices  14.3 us (24%)
  other arithmetic  13.9 us (24%)
  waiting for transfers between devices  13.4 us (23%)
    ppermute x3, waiting for transfers between devices, from_partner(): return lax.ppermute(value, axis, pairs)  12.8 us
    ppermute x2, starting transfers between devices, padded(): lax.ppermute(lax.slice_in_dim(block, 0, width, axis=dim), axis, backward)  8.19 us
    scatter x1, local copies, waits for them, and re-layouts, local(): extended = extended.at[:, :, rows_here + 1, 1:-1].set(north_row)  6.16 us
    ppermute x2, starting transfers between devices, padded(): lax.ppermute(lax.slice_in_dim(block, block.shape[dim] - width, None, axis...  3.28 us
    ppermute x3, starting transfers between devices, from_partner(): return lax.ppermute(value, axis, pairs)  2.84 us
    concatenate x1, other arithmetic, padded(): block = jnp.concatenate([low, block, high], axis=dim)  2.49 us
    unnamed x5, local copies, waits for them, and re-layouts  2.31 us
    slice x1, other arithmetic, padded(): lax.slice_in_dim(block, block.shape[dim] - width, None, axis=dim)  2.04 us
  transfers between devices with their start and end apart: 7, of which 3 were waited for; matrix products, arithmetic and copies ran while one was open for 20% of the time, Pallas kernels for 0%

commit v1 on v0

v1 whole, which is shorter than its diff:
```python
import functools

import jax
import jax.numpy as jnp
from jax import lax
from jax.experimental import pallas as pl
from jax.experimental.pallas import tpu as pltpu
from jax.sharding import PartitionSpec as P

THERMAL = 0.2
HALINE = 0.8
REDI = 0.1
SKEW = 0.05
SLOPE_MAX = 0.6
SLOPE_WIDTH = 0.2

MESH = pl.DeviceIdType.MESH
PAD = 8
HEAD = 8
PIECES = 5
C, E, W, N, S = range(5)


def taper(slope):
    return slope * 0.5 * (1.0 + jnp.tanh((SLOPE_MAX - jnp.abs(slope)) / SLOPE_WIDTH))


def shift_sum(values, k):
    above = values[k - 1] if k > 0 else None
    below = values[k] if k < len(values) else None
    return above, below


def total(*terms):
    terms = [term for term in terms if term is not None]
    result = terms[0]
    for term in terms[1:]:
        result = result + term
    return result


def coefficients(rho, kmt, levels):
    zero = jnp.zeros_like(kmt[C])
    wet, lm, cell = [], [], []
    for d in range(5):
        w = [(kmt[d] > float(k)).astype(jnp.float32) for k in range(levels)]
        m = [w[k + 1] * w[k] for k in range(levels - 1)]
        st = [(rho[d][k + 1] - rho[d][k]) * m[k] for k in range(levels - 1)]
        wet.append(w)
        lm.append(m)
        cell.append([0.5 * total(*shift_sum(st, k)) for k in range(levels)])
    mask = [None] + [[wet[C][k] * wet[d][k] for k in range(levels)] for d in (E, W, N, S)]
    slope = [None]
    for d in (E, W, N, S):
        sign = 1.0 if d in (E, N) else -1.0
        slope.append(
            [
                taper(
                    sign
                    * (rho[d][k] - rho[C][k])
                    * mask[d][k]
                    / jnp.maximum(0.5 * (cell[d][k] + cell[C][k]), 1.0)
                )
                for k in range(levels)
            ]
        )
    cx = [0.5 * (slope[W][k] + slope[E][k]) for k in range(levels)]
    cy = [0.5 * (slope[S][k] + slope[N][k]) for k in range(levels)]
    xs, ys, zs = [], [], []
    for k in range(levels - 1):
        sxw = 0.5 * (cx[k] + cx[k + 1])
        syw = 0.5 * (cy[k] + cy[k + 1])
        xs.append(((REDI + SKEW) * 0.25) * sxw * lm[C][k])
        ys.append(((REDI + SKEW) * 0.25) * syw * lm[C][k])
        zs.append(REDI * (sxw * sxw + syw * syw) * lm[C][k])
    out = {}
    for k in range(levels):
        first, last = k == 0, k == levels - 1
        centre, up, down = 1.0, zero, zero
        q = zero
        for d in (E, W, N, S):
            sign = 1.0 if d in (E, N) else -1.0
            face = xs if d in (E, W) else ys
            p = (sign * (REDI - SKEW) * 0.25) * slope[d][k] * mask[d][k]
            q = q + p
            lo = zero if first else lm[d][k - 1]
            hi = zero if last else lm[d][k]
            flo = zero if first else face[k - 1]
            fhi = zero if last else face[k]
            own = sign * mask[d][k] * (fhi - flo)
            out[d, k, 1] = REDI * mask[d][k] + p * (lo - hi) + own
            out[d, k, 2] = zero if last else p * hi + sign * mask[d][k + 1] * fhi
            out[d, k, 0] = zero if first else -p * lo - sign * mask[d][k - 1] * flo
            centre = centre - REDI * mask[d][k] - own
            if not last:
                up = up - sign * mask[d][k + 1] * fhi
            if not first:
                down = down + sign * mask[d][k - 1] * flo
        lo = zero if first else lm[C][k - 1]
        hi = zero if last else lm[C][k]
        zlo = zero if first else zs[k - 1]
        zhi = zero if last else zs[k]
        out[C, k, 1] = centre + q * (lo - hi) - (zhi + zlo)
        out[C, k, 2] = up + q * hi + zhi
        out[C, k, 0] = down - q * lo + zlo
    return out


def kernel(
    sizes, x_ref, kmt_ref, out_ref,
    xv, coef, edge, cols, west, east, merged, north, south, from_n, from_s,
    load_sem, send_sem, recv_sem,
):
    tracers, levels, rows, lanes, n_lon, n_lat = sizes
    lon, lat = lax.axis_index("lon"), lax.axis_index("lat")
    at_top = lat == n_lat - 1
    inner = lat > 0
    e_dev = (lax.rem(lon + 1, n_lon), lat)
    w_dev = (lax.rem(lon + n_lon - 1, n_lon), lat)
    fold_dev = (n_lon - 1 - lon, lat)
    plane = levels * rows
    per_reg = lanes // 2

    barrier = pltpu.get_barrier_semaphore()

    def greet(dev):
        pl.semaphore_signal(barrier, inc=1, device_id=dev, device_id_type=MESH)

    @pl.when(at_top)
    def _():
        greet(fold_dev)

    @pl.when(jnp.logical_not(at_top))
    def _():
        greet((lon, lat + 1))

    greet(e_dev)
    greet(w_dev)

    @pl.when(inner)
    def _():
        greet((lon, lat - 1))

    step = tracers // PIECES * plane
    loads = []
    for i in range(PIECES):
        copy = pltpu.make_async_copy(
            x_ref.at[pl.ds(i * step, step)], xv.at[pl.ds(PAD + i * step, step)], load_sem.at[i]
        )
        copy.start()
        loads.append(copy)

    zeros = jnp.zeros((8, lanes), jnp.float32)
    xv[pl.ds(0, PAD), :] = zeros
    xv[pl.ds(PAD + tracers * plane, PAD), :] = zeros
    lane = lax.broadcasted_iota(jnp.int32, (8, lanes), 1)
    row = lax.broadcasted_iota(jnp.int32, (8, lanes), 0)
    half = lane // 2
    even = lane % 2 == 0

    kmt_own = kmt_ref[...].astype(jnp.float32)
    north[pl.ds(0, HEAD), :] = jnp.broadcast_to(kmt_own[rows - 1 : rows, :], (HEAD, lanes))
    south[pl.ds(0, HEAD), :] = jnp.broadcast_to(kmt_own[0:1, :], (HEAD, lanes))
    regs = tracers * levels // per_reg
    cols[pl.ds(regs * 8, 8), :] = pltpu.roll(kmt_own, 1, 1)

    group = per_reg // levels
    per_piece = tracers // PIECES
    for i in range(PIECES):
        loads[i].wait()

        @pl.loop(i * per_piece, (i + 1) * per_piece)
        def _(t):
            base = PAD + t * plane
            north[pl.ds(HEAD + t * levels, levels), :] = xv[pl.ds(base + rows - 1, levels, stride=rows), :]
            south[pl.ds(HEAD + t * levels, levels), :] = xv[pl.ds(base, levels, stride=rows), :]

        for v in range(i * per_piece // group, (i + 1) * per_piece // group):
            acc = zeros
            for q in range(per_reg):
                value = xv[pl.ds(PAD + (v * per_reg + q) * rows, rows), :]
                acc = jnp.where(half == q, pltpu.roll(value, (2 * q + 1) % lanes, 1), acc)
            cols[pl.ds(v * 8, 8), :] = acc

    @pl.when(inner)
    def _():
        pl.semaphore_wait(barrier, 4)

    @pl.when(jnp.logical_not(inner))
    def _():
        pl.semaphore_wait(barrier, 3)

    small = HEAD + 2 * levels
    big = (tracers - 2) * levels

    def send(src, dst, rows_at, count, s, r, dev):
        return pltpu.make_async_remote_copy(
            src_ref=src.at[pl.ds(rows_at, count)],
            dst_ref=dst.at[pl.ds(rows_at, count)],
            send_sem=send_sem.at[s],
            recv_sem=recv_sem.at[r],
            device_id=dev,
            device_id_type=MESH,
        )

    everything = (regs + 1) * 8
    fold = [send(north, from_n, 0, small, 0, 0, fold_dev), send(north, from_n, small, big, 1, 1, fold_dev)]
    to_n = [send(north, from_s, 0, small, 0, 2, (lon, lat + 1)), send(north, from_s, small, big, 1, 3, (lon, lat + 1))]
    to_s = [send(south, from_n, 0, small, 2, 0, (lon, lat - 1)), send(south, from_n, small, big, 3, 1, (lon, lat - 1))]
    to_e = send(cols, west, 0, everything, 4, 4, e_dev)
    to_w = send(cols, east, 0, everything, 5, 5, w_dev)
    for part in range(2):

        @pl.when(at_top)
        def _():
            fold[part].start()

        @pl.when(jnp.logical_not(at_top))
        def _():
            to_n[part].start()

        @pl.when(inner)
        def _():
            to_s[part].start()

        if part == 0:
            to_e.start()
            to_w.start()

    @pl.when(jnp.logical_not(inner))
    def _():
        for i in range(small // 8):
            from_s[pl.ds(i * 8, 8), :] = zeros

    to_e.wait_recv()
    to_w.wait_recv()
    for v in range(regs + 1):
        merged[pl.ds(v * 8, 8), :] = jnp.where(even, west[pl.ds(v * 8, 8), :], east[pl.ds(v * 8, 8), :])

    def beside(value, halo, shift):
        m = pltpu.roll(halo, shift, 1)
        e = pltpu.roll(jnp.where(lane == 0, m, value), lanes - 1, 1)
        w = pltpu.roll(jnp.where(lane == lanes - 1, m, value), 1, 1)
        return e, w

    def flipped(value):
        turned = jnp.take_along_axis(value, lanes - 1 - lane, axis=1)
        return jnp.where(at_top, turned, value)

    fold[0].wait_recv()

    @pl.when(inner)
    def _():
        to_n[0].wait_recv()

    rho = [[], [], [], [], []]
    rho_n = flipped(
        HALINE * from_n[pl.ds(HEAD + levels, levels), :] - THERMAL * from_n[pl.ds(HEAD, levels), :]
    )
    rho_s = HALINE * from_s[pl.ds(HEAD + levels, levels), :] - THERMAL * from_s[pl.ds(HEAD, levels), :]
    rho_h = HALINE * pltpu.roll(merged[pl.ds(0, 8), :], lanes - 2 * levels, 1) - THERMAL * merged[pl.ds(0, 8), :]

    def north_of(value, halo):
        return jnp.where(row == rows - 1, halo, pltpu.roll(value, rows - 1, 0))

    def south_of(value, halo):
        return jnp.where(row == 0, halo, pltpu.roll(value, 1, 0))

    for k in range(levels):
        own = HALINE * xv[pl.ds(PAD + plane + k * rows, rows), :] - THERMAL * xv[pl.ds(PAD + k * rows, rows), :]
        e, w = beside(own, rho_h, (lanes - (2 * k + 1)) % lanes)
        rho[C].append(own)
        rho[E].append(e)
        rho[W].append(w)
        rho[N].append(north_of(own, jnp.broadcast_to(rho_n[k : k + 1, :], (rows, lanes))))
        rho[S].append(south_of(own, jnp.broadcast_to(rho_s[k : k + 1, :], (rows, lanes))))
    kmt_e, kmt_w = beside(kmt_own, merged[pl.ds(regs * 8, 8), :], lanes - 1)
    kmts = [
        kmt_own, kmt_e, kmt_w,
        north_of(kmt_own, flipped(from_n[pl.ds(0, 8), :])),
        south_of(kmt_own, from_s[pl.ds(0, 8), :]),
    ]
    table = coefficients(rho, kmts, levels)
    for (d, k, dk), value in table.items():
        coef[pl.ds(((d * 3 + dk) * levels + k) * 8, 8), :] = value
    for slot, (d, at) in enumerate(((N, rows - 1), (S, 0))):
        for dk in range(3):
            place = pl.ds((d * 3 + dk) * plane + at, levels, stride=rows)
            edge[pl.ds((slot * 3 + dk) * 8, 8), :] = coef[place, :]
            coef[place, :] = zeros

    def piece(d, dk, k):
        return coef[pl.ds(((d * 3 + dk) * levels + k) * 8, 8), :]

    together = 2

    @pl.loop(0, tracers // together)
    def _(pair):
        fields = []
        for u in range(together):
            t = pair * together + u
            base = PAD + t * plane
            p0 = t * levels
            reg = merged[pl.ds(pl.multiple_of(p0 // per_reg * 8, 8), 8), :]
            reg = pltpu.roll(reg, lax.rem(lanes - 2 * lax.rem(p0, per_reg) - 1 + lanes, lanes), 1)
            field = []
            for k in range(levels):
                own = xv[pl.ds(pl.multiple_of(base + k * rows, 8), rows), :]
                e, w = beside(own, reg, (lanes - 2 * k) % lanes)
                n = pltpu.roll(own, rows - 1, 0)
                s = pltpu.roll(own, 1, 0)
                field.append((own, e, w, n, s))
            fields.append(field)
        for k in range(levels):
            sums = [None] * together
            for d in range(5):
                for dk in range(3):
                    if not 0 <= k + dk - 1 < levels:
                        continue
                    c = piece(d, dk, k)
                    for u in range(together):
                        term = c * fields[u][k + dk - 1][d]
                        sums[u] = term if sums[u] is None else sums[u] + term
            for u in range(together):
                t = pair * together + u
                out_ref[pl.ds(pl.multiple_of(t * plane + k * rows, 8), rows), :] = sums[u]

    def fix(slot, source, at, turn):
        cs = [edge[pl.ds((slot * 3 + dk) * 8, 8), :] for dk in range(3)]

        @pl.loop(0, tracers, unroll=4)
        def _(t):
            h = source[pl.ds(pl.multiple_of(HEAD + t * levels, 8), levels), :]
            if turn:
                h = flipped(h)
            add = cs[1] * h + cs[2] * pltpu.roll(h, levels - 1, 0) + cs[0] * pltpu.roll(h, 1, 0)
            place = pl.ds(t * plane + at, levels, stride=rows)
            out_ref[place, :] = out_ref[place, :] + add

    @pl.when(inner)
    def _():
        to_n[1].wait_recv()
        fix(1, from_s, 0, False)

    fold[1].wait_recv()
    fix(0, from_n, rows - 1, True)

    for part in range(2):
        fold[part].wait_send()

        @pl.when(inner)
        def _():
            to_s[part].wait_send()

    to_e.wait_send()
    to_w.wait_send()


def solution(mesh):
    n_lon, n_lat = mesh.shape["lon"], mesh.shape["lat"]

    def local(tracers, kmt):
        nt, levels, rows, lanes = tracers.shape
        flat = tracers.reshape(nt * levels * rows, lanes)
        total_rows = nt * levels * rows
        packed = (nt * levels * 2 // lanes + 1) * 8
        halo = HEAD + nt * levels

        def vmem(*shape):
            return pltpu.VMEM(shape, jnp.float32)

        out = pl.pallas_call(
            functools.partial(kernel, (nt, levels, rows, lanes, n_lon, n_lat)),
            out_shape=jax.ShapeDtypeStruct((total_rows, lanes), jnp.float32),
            in_specs=[pl.BlockSpec(memory_space=pl.ANY), pl.BlockSpec(memory_space=pltpu.VMEM)],
            out_specs=pl.BlockSpec(memory_space=pltpu.VMEM),
            scratch_shapes=[
                vmem(total_rows + 2 * PAD, lanes),
                vmem(15 * levels * 8, lanes),
                vmem(6 * 8, lanes),
                vmem(packed, lanes),
                vmem(packed, lanes),
                vmem(packed, lanes),
                vmem(packed, lanes),
                vmem(halo, lanes),
                vmem(halo, lanes),
                vmem(halo, lanes),
                vmem(halo, lanes),
                pltpu.SemaphoreType.DMA((PIECES,)),
                pltpu.SemaphoreType.DMA((6,)),
                pltpu.SemaphoreType.DMA((6,)),
            ],
            compiler_params=pltpu.CompilerParams(collective_id=0, has_side_effects=True),
        )(flat, kmt)
        return out.reshape(nt, levels, rows, lanes)

    return jax.shard_map(
        local,
        mesh=mesh,
        in_specs=(P(None, None, "lat", "lon"), P("lat", "lon")),
        out_specs=P(None, None, "lat", "lon"),
        check_vma=False,
    )
```

time: 58.6 us -> 20.6 us (0.35)
  the two profiles are of different devices: /device:TPU:1 before, /device:TPU:0 now
where the time goes in v1:
time: 20.6 us; the launch traced here: 20.4 us
  Pallas kernels  17.9 us (87%)
  local copies, waits for them, and re-layouts  2.52 us (12%)
    pallas_call x1, Pallas kernels, local(): pl.pallas_call(functools.partial(kernel, (nt, levels, rows, lanes, n_lon,...  17.9 us
    unnamed x1, local copies, waits for them, and re-layouts  2.52 us

profile of v1, /device:TPU:0, one launch (start us, length us, event | category | flops | bytes accessed | tf_op | source)
XLA Modules:
  0.0 20.4 jit_solution(17369574018635905070)
XLA Ops:
  0.0 17.9 %shard_map.28 = f32[2560,128]{1,0:T(8,128)} custom-call(f32[2560,128]{1,0:T(8,128)} %bitcast.3, s32[8,128]{1,0:T(8,128)} %kmt_ref.1), custom_call_target="tpu_custom_call" | custom-call | tf_op jit(solution)/shard_map/pallas_call | solution.py:372
  17.9 2.5 %copy.4 = f32[40,8,8,128]{3,2,1,0:T(8,128)} copy(f32[40,8,8,128]{3,2,1,0:T(8,128)} %bitcast.2) | data formatting | bytes 2621440

commit v2 on v1

v2 whole, which is shorter than its diff:
```python
import functools

import jax
import jax.numpy as jnp
from jax import lax
from jax.experimental import pallas as pl
from jax.experimental.pallas import tpu as pltpu
from jax.sharding import PartitionSpec as P

THERMAL = 0.2
HALINE = 0.8
REDI = 0.1
SKEW = 0.05
SLOPE_MAX = 0.6
SLOPE_WIDTH = 0.2

MESH = pl.DeviceIdType.MESH
PAD = 8
HEAD = 8
TOGETHER = 2
UNALIGNED = False
C, E, W, N, S = range(5)


def taper(slope):
    return slope * 0.5 * (1.0 + jnp.tanh((SLOPE_MAX - jnp.abs(slope)) / SLOPE_WIDTH))


def shift_sum(values, k):
    above = values[k - 1] if k > 0 else None
    below = values[k] if k < len(values) else None
    return above, below


def total(*terms):
    terms = [term for term in terms if term is not None]
    result = terms[0]
    for term in terms[1:]:
        result = result + term
    return result


def coefficients(rho, kmt, levels):
    zero = jnp.zeros_like(kmt[C])
    wet, lm, cell = [], [], []
    for d in range(5):
        w = [(kmt[d] > float(k)).astype(jnp.float32) for k in range(levels)]
        m = [w[k + 1] * w[k] for k in range(levels - 1)]
        st = [(rho[d][k + 1] - rho[d][k]) * m[k] for k in range(levels - 1)]
        wet.append(w)
        lm.append(m)
        cell.append([0.5 * total(*shift_sum(st, k)) for k in range(levels)])
    mask = [None] + [[wet[C][k] * wet[d][k] for k in range(levels)] for d in (E, W, N, S)]
    slope = [None]
    for d in (E, W, N, S):
        sign = 1.0 if d in (E, N) else -1.0
        slope.append(
            [
                taper(
                    sign
                    * (rho[d][k] - rho[C][k])
                    * mask[d][k]
                    / jnp.maximum(0.5 * (cell[d][k] + cell[C][k]), 1.0)
                )
                for k in range(levels)
            ]
        )
    cx = [0.5 * (slope[W][k] + slope[E][k]) for k in range(levels)]
    cy = [0.5 * (slope[S][k] + slope[N][k]) for k in range(levels)]
    xs, ys, zs = [], [], []
    for k in range(levels - 1):
        sxw = 0.5 * (cx[k] + cx[k + 1])
        syw = 0.5 * (cy[k] + cy[k + 1])
        xs.append(((REDI + SKEW) * 0.25) * sxw * lm[C][k])
        ys.append(((REDI + SKEW) * 0.25) * syw * lm[C][k])
        zs.append(REDI * (sxw * sxw + syw * syw) * lm[C][k])
    out = {}
    for k in range(levels):
        first, last = k == 0, k == levels - 1
        centre, up, down = 1.0, zero, zero
        q = zero
        for d in (E, W, N, S):
            sign = 1.0 if d in (E, N) else -1.0
            face = xs if d in (E, W) else ys
            p = (sign * (REDI - SKEW) * 0.25) * slope[d][k] * mask[d][k]
            q = q + p
            lo = zero if first else lm[d][k - 1]
            hi = zero if last else lm[d][k]
            flo = zero if first else face[k - 1]
            fhi = zero if last else face[k]
            own = sign * mask[d][k] * (fhi - flo)
            out[d, k, 1] = REDI * mask[d][k] + p * (lo - hi) + own
            out[d, k, 2] = zero if last else p * hi + sign * mask[d][k + 1] * fhi
            out[d, k, 0] = zero if first else -p * lo - sign * mask[d][k - 1] * flo
            centre = centre - REDI * mask[d][k] - own
            if not last:
                up = up - sign * mask[d][k + 1] * fhi
            if not first:
                down = down + sign * mask[d][k - 1] * flo
        lo = zero if first else lm[C][k - 1]
        hi = zero if last else lm[C][k]
        zlo = zero if first else zs[k - 1]
        zhi = zero if last else zs[k]
        out[C, k, 1] = centre + q * (lo - hi) - (zhi + zlo)
        out[C, k, 2] = up + q * hi + zhi
        out[C, k, 0] = down - q * lo + zlo
    return out


def kernel(
    sizes, x_ref, kmt_ref, out_ref,
    xv, kmt_own_ref, coef, edge, cols, west, east, north, south, from_n, from_s,
    load_sem, send_sem, recv_sem,
):
    tracers, levels, rows, lanes, n_lon, n_lat = sizes
    lon, lat = lax.axis_index("lon"), lax.axis_index("lat")
    at_top = lat == n_lat - 1
    below_top = jnp.logical_not(at_top)
    inner = lat > 0
    e_dev = (lax.rem(lon + 1, n_lon), lat)
    w_dev = (lax.rem(lon + n_lon - 1, n_lon), lat)
    fold_dev = (n_lon - 1 - lon, lat)
    plane = levels * rows
    per_reg = lanes // 2
    group = per_reg // levels
    pieces = tracers // group
    step = group * plane

    barrier = pltpu.get_barrier_semaphore()

    def greet(dev):
        pl.semaphore_signal(barrier, inc=1, device_id=dev, device_id_type=MESH)

    with jax.named_scope("greet"):

        @pl.when(at_top)
        def _():
            greet(fold_dev)

        @pl.when(below_top)
        def _():
            greet((lon, lat + 1))

        greet(e_dev)
        greet(w_dev)

        @pl.when(inner)
        def _():
            greet((lon, lat - 1))

    load_kmt = pltpu.make_async_copy(kmt_ref, kmt_own_ref, load_sem.at[pieces])
    load_kmt.start()
    loads = []
    for i in range(pieces):
        copy = pltpu.make_async_copy(
            x_ref.at[pl.ds(i * step, step)], xv.at[pl.ds(PAD + i * step, step)], load_sem.at[i]
        )
        copy.start()
        loads.append(copy)

    zeros = jnp.zeros((8, lanes), jnp.float32)
    xv[pl.ds(0, PAD), :] = zeros
    xv[pl.ds(PAD + tracers * plane, PAD), :] = zeros
    lane = lax.broadcasted_iota(jnp.int32, (8, lanes), 1)
    row = lax.broadcasted_iota(jnp.int32, (8, lanes), 0)
    even = lane % 2 == 0
    spot = (lane + 1) % lanes // 2
    backwards = lanes - 1 - lane
    from_east, from_west = lane == lanes - 1, lane == 0

    def flipped(value):
        return jnp.take_along_axis(value, backwards, axis=1)

    def pack_cols(i):
        acc = zeros
        for q in range(per_reg):
            value = xv[pl.ds(PAD + (i * per_reg + q) * rows, rows), :]
            if q:
                value = pltpu.roll(value, 2 * q, 1)
            acc = jnp.where(spot == q, value, acc)
        cols[pl.ds(8 + i * 8, 8), :] = acc

    def pack_rows(first, last):
        for t in range(first, last):
            base = PAD + t * plane
            n = xv[pl.ds(base + rows - 1, levels, stride=rows), :]
            north[pl.ds(HEAD + t * levels, levels), :] = n
            south[pl.ds(HEAD + t * levels, levels), :] = xv[pl.ds(base, levels, stride=rows), :]

    def turn_rows(first, count):
        @pl.when(at_top)
        def _():
            for i in range(first // 8, (first + count) // 8):
                north[pl.ds(i * 8, 8), :] = flipped(north[pl.ds(i * 8, 8), :])

    small = HEAD + 2 * levels
    big = (tracers - 2) * levels

    with jax.named_scope("pack0"):
        load_kmt.wait()
        kmt_own = kmt_own_ref[...].astype(jnp.float32)
        north[pl.ds(0, HEAD), :] = jnp.broadcast_to(kmt_own[rows - 1 : rows, :], (HEAD, lanes))
        south[pl.ds(0, HEAD), :] = jnp.broadcast_to(kmt_own[0:1, :], (HEAD, lanes))
        cols[pl.ds(0, 8), :] = kmt_own
        loads[0].wait()
        pack_rows(0, 2)
        turn_rows(0, small)
        pack_cols(0)

    with jax.named_scope("barrier"):

        @pl.when(inner)
        def _():
            pl.semaphore_wait(barrier, 4)

        @pl.when(jnp.logical_not(inner))
        def _():
            pl.semaphore_wait(barrier, 3)

    def send(src, dst, rows_at, count, s, dev, r=None):
        return pltpu.make_async_remote_copy(
            src_ref=src.at[pl.ds(rows_at, count)],
            dst_ref=dst.at[pl.ds(rows_at, count)],
            send_sem=send_sem.at[s],
            recv_sem=recv_sem.at[s if r is None else r],
            device_id=dev,
            device_id_type=MESH,
        )

    spans = ((0, small), (small, big))
    fold = [send(north, from_n, *spans[i], 2 + i, fold_dev, i) for i in range(2)]
    to_n = [send(north, from_s, *spans[i], 2 + i, (lon, lat + 1)) for i in range(2)]
    to_s = [send(south, from_n, *spans[i], i, (lon, lat - 1)) for i in range(2)]

    def columns(first, count, i):
        return (
            send(cols, west, first, count, 4 + 2 * i, e_dev),
            send(cols, east, first, count, 5 + 2 * i, w_dev),
        )

    def piece_columns(i):
        return columns(8 + i * 8, 8, i)

    def send_rows(part):
        @pl.when(at_top)
        def _():
            fold[part].start()

        @pl.when(below_top)
        def _():
            to_n[part].start()

        @pl.when(inner)
        def _():
            to_s[part].start()

    head_cols = columns(0, 16, 0)
    with jax.named_scope("send"):
        send_rows(0)
        for copy in head_cols:
            copy.start()
    with jax.named_scope("pack"):
        for i in range(1, pieces):
            loads[i].wait()
            pack_cols(i)
            for copy in piece_columns(i):
                copy.start()
        pack_rows(2, tracers)
        turn_rows(small, big)
        send_rows(1)

    with jax.named_scope("waitsmall"):

        @pl.when(jnp.logical_not(inner))
        def _():
            for i in range(small // 8):
                from_s[pl.ds(i * 8, 8), :] = zeros

        fold[0].wait_recv()

        @pl.when(inner)
        def _():
            to_n[0].wait_recv()

        for copy in head_cols:
            copy.wait_recv()

    def merged(at):
        return jnp.where(even, east[pl.ds(at, 8), :], pltpu.roll(west[pl.ds(at, 8), :], 2, 1))

    def beside(value, halo):
        e = jnp.where(from_east, halo, pltpu.roll(value, lanes - 1, 1))
        w = jnp.where(from_west, halo, pltpu.roll(value, 1, 1))
        return e, w

    def north_of(value, halo):
        return jnp.where(row == rows - 1, halo, pltpu.roll(value, rows - 1, 0))

    def south_of(value, halo):
        return jnp.where(row == 0, halo, pltpu.roll(value, 1, 0))

    with jax.named_scope("coefs"):
        rho = [[], [], [], [], []]
        rho_n = HALINE * from_n[pl.ds(HEAD + levels, levels), :] - THERMAL * from_n[pl.ds(HEAD, levels), :]
        rho_s = HALINE * from_s[pl.ds(HEAD + levels, levels), :] - THERMAL * from_s[pl.ds(HEAD, levels), :]
        reg = merged(8)
        rho_h = HALINE * pltpu.roll(reg, lanes - 2 * levels, 1) - THERMAL * reg
        for k in range(levels):
            own = HALINE * xv[pl.ds(PAD + plane + k * rows, rows), :] - THERMAL * xv[pl.ds(PAD + k * rows, rows), :]
            e, w = beside(own, pltpu.roll(rho_h, lanes - 2 * k - 1, 1))
            rho[C].append(own)
            rho[E].append(e)
            rho[W].append(w)
            rho[N].append(north_of(own, jnp.broadcast_to(rho_n[k : k + 1, :], (rows, lanes))))
            rho[S].append(south_of(own, jnp.broadcast_to(rho_s[k : k + 1, :], (rows, lanes))))
        kmts = [
            kmt_own,
            jnp.where(from_east, pltpu.roll(east[pl.ds(0, 8), :], lanes - 1, 1), pltpu.roll(kmt_own, lanes - 1, 1)),
            jnp.where(from_west, pltpu.roll(west[pl.ds(0, 8), :], 1, 1), pltpu.roll(kmt_own, 1, 1)),
            north_of(kmt_own, from_n[pl.ds(0, 8), :]),
            south_of(kmt_own, from_s[pl.ds(0, 8), :]),
        ]
        table = coefficients(rho, kmts, levels)
        for (d, k, dk), value in table.items():
            coef[pl.ds(((d * 3 + dk) * levels + k) * 8, 8), :] = value
        for slot, (d, at) in enumerate(((N, rows - 1), (S, 0))):
            for dk in range(3):
                place = pl.ds((d * 3 + dk) * plane + at, levels, stride=rows)
                edge[pl.ds((slot * 3 + dk) * 8, 8), :] = coef[place, :]
                coef[place, :] = zeros

    def piece(d, dk, k):
        return coef[pl.ds(((d * 3 + dk) * levels + k) * 8, 8), :]

    together = TOGETHER

    def batch(reg, i, first):
        fields = []
        for u in range(together):
            t = i * group + first + u
            base = pl.multiple_of(PAD + t * plane, 8)
            field = []
            for k in range(levels):
                own = xv[pl.ds(base + k * rows, rows), :]
                halo = pltpu.roll(reg, (2 * lanes - 2 * ((first + u) * levels + k) - 1) % lanes, 1)
                e, w = beside(own, halo)
                if UNALIGNED:
                    n = xv[pl.ds(base + k * rows + 1, rows), :]
                    s = xv[pl.ds(base + k * rows - 1, rows), :]
                else:
                    n = pltpu.roll(own, rows - 1, 0)
                    s = pltpu.roll(own, 1, 0)
                field.append((own, e, w, n, s))
            fields.append(field)
        for k in range(levels):
            sums = [None] * together
            for d in range(5):
                for dk in range(3):
                    if not 0 <= k + dk - 1 < levels:
                        continue
                    c = piece(d, dk, k)
                    for u in range(together):
                        term = c * fields[u][k + dk - 1][d]
                        sums[u] = term if sums[u] is None else sums[u] + term
            for u in range(together):
                t = i * group + first + u
                out_ref[pl.ds(pl.multiple_of(t * plane + k * rows, 8), rows), :] = sums[u]

    with jax.named_scope("main"):

        @pl.loop(0, pieces)
        def _(i):
            @pl.when(i > 0)
            def _():
                for copy in piece_columns(i):
                    copy.wait_recv()

            reg = merged(pl.multiple_of(8 + i * 8, 8))
            for first in range(0, group, together):
                batch(reg, i, first)

    def fix(slot, source, at):
        cs = [edge[pl.ds((slot * 3 + dk) * 8, 8), :] for dk in range(3)]

        @pl.loop(0, pieces)
        def _(i):
            for u in range(group):
                t = i * group + u
                h = source[pl.ds(pl.multiple_of(HEAD + t * levels, 8), levels), :]
                add = cs[1] * h + cs[2] * pltpu.roll(h, levels - 1, 0) + cs[0] * pltpu.roll(h, 1, 0)
                place = pl.ds(t * plane + at, levels, stride=rows)
                out_ref[place, :] = out_ref[place, :] + add

    with jax.named_scope("fixs"):

        @pl.when(inner)
        def _():
            to_n[1].wait_recv()
            fix(1, from_s, 0)

    with jax.named_scope("waitbig"):
        fold[1].wait_recv()
    with jax.named_scope("fixn"):
        fix(0, from_n, rows - 1)

    with jax.named_scope("end"):
        for part in range(2):
            fold[part].wait_send()

            @pl.when(inner)
            def _():
                to_s[part].wait_send()

        for copy in head_cols:
            copy.wait_send()
        for i in range(1, pieces):
            for copy in piece_columns(i):
                copy.wait_send()


def solution(mesh):
    n_lon, n_lat = mesh.shape["lon"], mesh.shape["lat"]

    def local(tracers, kmt):
        nt, levels, rows, lanes = tracers.shape
        flat = tracers.reshape(nt * levels * rows, lanes)
        total_rows = nt * levels * rows
        pieces = nt * levels * 2 // lanes
        packed = (pieces + 1) * 8
        halo = HEAD + nt * levels

        def vmem(*shape):
            return pltpu.VMEM(shape, jnp.float32)

        out = pl.pallas_call(
            functools.partial(kernel, (nt, levels, rows, lanes, n_lon, n_lat)),
            out_shape=pltpu.VMEM((total_rows, lanes), jnp.float32),
            in_specs=[pl.BlockSpec(memory_space=pltpu.HBM), pl.BlockSpec(memory_space=pltpu.HBM)],
            out_specs=pl.BlockSpec(memory_space=pltpu.VMEM),
            scratch_shapes=[
                vmem(total_rows + 2 * PAD, lanes),
                pltpu.VMEM((rows, lanes), jnp.int32),
                vmem(15 * levels * 8, lanes),
                vmem(6 * 8, lanes),
                vmem(packed, lanes),
                vmem(packed, lanes),
                vmem(packed, lanes),
                vmem(halo, lanes),
                vmem(halo, lanes),
                vmem(halo, lanes),
                vmem(halo, lanes),
                pltpu.SemaphoreType.DMA((pieces + 1,)),
                pltpu.SemaphoreType.DMA((4 + 2 * pieces,)),
                pltpu.SemaphoreType.DMA((4 + 2 * pieces,)),
            ],
            compiler_params=pltpu.CompilerParams(collective_id=0, has_side_effects=True),
        )(flat, kmt)
        return out.reshape(nt, levels, rows, lanes)

    return jax.shard_map(
        local,
        mesh=mesh,
        in_specs=(P(None, None, "lat", "lon"), P("lat", "lon")),
        out_specs=P(None, None, "lat", "lon"),
        check_vma=False,
    )
```

time: 20.6 us -> 12.9 us (0.63)
  the two profiles are of different devices: /device:TPU:0 before, /device:TPU:1 now
where the time goes in v2:
time: 12.9 us; the launch traced here: 12.7 us
  Pallas kernels  11.6 us (90%)
  local copies, waits for them, and re-layouts  1.06 us (8%)
    pallas_call x1, Pallas kernels, local(): pl.pallas_call(functools.partial(kernel, (nt, levels, rows, lanes, n_lon,...  11.6 us
    unnamed x1, local copies, waits for them, and re-layouts  1.06 us

profile of v2, /device:TPU:1, one launch (start us, length us, event | category | flops | bytes accessed | tf_op | source)
XLA Modules:
  0.0 12.7 jit_solution(2184803509028030714)
XLA Ops:
  0.0 11.6 %shard_map.28 = f32[2560,128]{1,0:T(8,128)S(1)} custom-call(f32[2560,128]{1,0:T(8,128)} %bitcast.3, s32[8,128]{1,0:T(8,128)} %kmt_ref.1), custom_call_target="tpu_custom_call" | custom-call | tf_op jit(solution)/shard_map/pallas_call | solution.py:435
  11.6 1.1 %copy.4 = f32[40,8,8,128]{3,2,1,0:T(8,128)} copy(f32[40,8,8,128]{3,2,1,0:T(8,128)S(1)} %bitcast.2) | data formatting | bytes 2621440

commit v3 on v2

--- a/solution.py
+++ b/solution.py
@@ -148,12 +148,13 @@
         def _():
             greet((lon, lat - 1))
 
-    load_kmt = pltpu.make_async_copy(kmt_ref, kmt_own_ref, load_sem.at[pieces])
+    load_kmt = pltpu.make_async_copy(kmt_ref, kmt_own_ref, load_sem.at[pieces + 1])
     load_kmt.start()
     loads = []
-    for i in range(pieces):
+    cuts = [0, 2 * plane] + [i * step for i in range(1, pieces + 1)]
+    for i, (first, last) in enumerate(zip(cuts, cuts[1:])):
         copy = pltpu.make_async_copy(
-            x_ref.at[pl.ds(i * step, step)], xv.at[pl.ds(PAD + i * step, step)], load_sem.at[i]
+            x_ref.at[pl.ds(first, last - first)], xv.at[pl.ds(PAD + first, last - first)], load_sem.at[i]
         )
         copy.start()
         loads.append(copy)
@@ -171,14 +172,14 @@
     def flipped(value):
         return jnp.take_along_axis(value, backwards, axis=1)
 
-    def pack_cols(i):
+    def pack_cols(i, count, to):
         acc = zeros
-        for q in range(per_reg):
+        for q in range(count):
             value = xv[pl.ds(PAD + (i * per_reg + q) * rows, rows), :]
             if q:
                 value = pltpu.roll(value, 2 * q, 1)
             acc = jnp.where(spot == q, value, acc)
-        cols[pl.ds(8 + i * 8, 8), :] = acc
+        cols[pl.ds(to, 8), :] = acc
 
     def pack_rows(first, last):
         for t in range(first, last):
@@ -205,7 +206,7 @@
         loads[0].wait()
         pack_rows(0, 2)
         turn_rows(0, small)
-        pack_cols(0)
+        pack_cols(0, 2 * levels, 8)
 
     with jax.named_scope("barrier"):
 
@@ -239,7 +240,7 @@
         )
 
     def piece_columns(i):
-        return columns(8 + i * 8, 8, i)
+        return columns(16 + i * 8, 8, 1 + i)
 
     def send_rows(part):
         @pl.when(at_top)
@@ -260,9 +261,9 @@
         for copy in head_cols:
             copy.start()
     with jax.named_scope("pack"):
-        for i in range(1, pieces):
-            loads[i].wait()
-            pack_cols(i)
+        for i in range(pieces):
+            loads[1 + i].wait()
+            pack_cols(i, per_reg, 16 + i * 8)
             for copy in piece_columns(i):
                 copy.start()
         pack_rows(2, tracers)
@@ -370,12 +371,9 @@
 
         @pl.loop(0, pieces)
         def _(i):
-            @pl.when(i > 0)
-            def _():
-                for copy in piece_columns(i):
-                    copy.wait_recv()
-
-            reg = merged(pl.multiple_of(8 + i * 8, 8))
+            for copy in piece_columns(i):
+                copy.wait_recv()
+            reg = merged(pl.multiple_of(16 + i * 8, 8))
             for first in range(0, group, together):
                 batch(reg, i, first)
 
@@ -413,7 +411,7 @@
 
         for copy in head_cols:
             copy.wait_send()
-        for i in range(1, pieces):
+        for i in range(pieces):
             for copy in piece_columns(i):
                 copy.wait_send()
 
@@ -426,7 +424,7 @@
         flat = tracers.reshape(nt * levels * rows, lanes)
         total_rows = nt * levels * rows
         pieces = nt * levels * 2 // lanes
-        packed = (pieces + 1) * 8
+        packed = (pieces + 2) * 8
         halo = HEAD + nt * levels
 
         def vmem(*shape):
@@ -449,9 +447,9 @@
                 vmem(halo, lanes),
                 vmem(halo, lanes),
                 vmem(halo, lanes),
-                pltpu.SemaphoreType.DMA((pieces + 1,)),
-                pltpu.SemaphoreType.DMA((4 + 2 * pieces,)),
-                pltpu.SemaphoreType.DMA((4 + 2 * pieces,)),
+                pltpu.SemaphoreType.DMA((pieces + 2,)),
+                pltpu.SemaphoreType.DMA((6 + 2 * pieces,)),
+                pltpu.SemaphoreType.DMA((6 + 2 * pieces,)),
             ],
             compiler_params=pltpu.CompilerParams(collective_id=0, has_side_effects=True),
         )(flat, kmt)

time: 12.9 us -> 12.9 us (level)
  no operation moved by 1% of the time
where the time goes in v3:
time: 12.9 us; the launch traced here: 12.7 us
  Pallas kernels  11.7 us (91%)
  local copies, waits for them, and re-layouts  1.06 us (8%)
    pallas_call x1, Pallas kernels, local(): pl.pallas_call(functools.partial(kernel, (nt, levels, rows, lanes, n_lon,...  11.7 us
    unnamed x1, local copies, waits for them, and re-layouts  1.06 us

profile of v3, /device:TPU:1, one launch (start us, length us, event | category | flops | bytes accessed | tf_op | source)
XLA Modules:
  0.0 12.7 jit_solution(140471968219429614)
XLA Ops:
  0.0 11.7 %shard_map.28 = f32[2560,128]{1,0:T(8,128)S(1)} custom-call(f32[2560,128]{1,0:T(8,128)} %bitcast.3, s32[8,128]{1,0:T(8,128)} %kmt_ref.1), custom_call_target="tpu_custom_call" | custom-call | tf_op jit(solution)/shard_map/pallas_call | solution.py:433
  11.7 1.1 %copy.4 = f32[40,8,8,128]{3,2,1,0:T(8,128)} copy(f32[40,8,8,128]{3,2,1,0:T(8,128)S(1)} %bitcast.2) | data formatting | bytes 2621440
